TPU v7x, 32 devices: a whole 2x2x4 slice. The times are simulated.
32 devices in a mesh: dev: 8 (over z, y), rep: 4 (over x, core).
Axes of the slice: x: 2, y: 2, z: 4, core: 2. Of those that a mesh axis runs over, the one named last changes fastest.
Arguments:
- features: bfloat16 [32768, 256], P(('dev', 'rep')), may hold values from -6 to 6
- history: bfloat16 [32768, 256], P(('dev', 'rep')), may hold values from -6 to 6
- new_owner: int32 [32, 8], P(('dev', 'rep')), may hold values from 0 to 7, as said below
- pull_rows: int32 [32768], P(('dev', 'rep')), may hold values from 0 to 1023
- occupancy: int32 [256, 16], P(('dev', 'rep')), may hold values from 0 to 1, as said below
- adj_local: bfloat16 [32768, 1024], P(('dev', 'rep')), may hold values from -0.125 to 0.125
- adj_boundary: bfloat16 [32768, 1024], P(('dev', 'rep')), may hold values from -0.125 to 0.125
- w_first: bfloat16 [256, 256], replicated, may hold values from -0.375 to 0.375
- bias_first: float32 [256], replicated, may hold values from -3 to 3
- w_second: bfloat16 [256, 256], replicated, may hold values from -0.375 to 0.375
- cotangent: bfloat16 [32768, 256], P(('dev', 'rep')), may hold values from -6 to 6
Outputs:
- hidden: bfloat16 [32768, 256], P(('dev', 'rep'))
- output: bfloat16 [32768, 256], P(('dev', 'rep'))
- w_second_grad: float32 [256, 256], replicated
Inputs may be any that keep to these rules, and one draw needn't show every extreme that they name: Each row of new_owner is a permutation of 0 to 7. `occupancy`: tile flags of 0 or 1.
All inputs are finite; a program needn't handle non-finite values.
Results may differ from a plain program's by a relative error of at most 0.0061.
Values may be sent and summed in bfloat16 or wider, within the bound.
A program may use at most 64 MiB of HBM per device.

v0:
```python
import jax
import jax.numpy as jnp
from jax import lax
from jax.sharding import PartitionSpec as P


def expand(occupied):
    return jnp.repeat(jnp.repeat(occupied, 128, axis=0), 128, axis=1).astype(jnp.bfloat16)


def dense_terms(owned, remote, adj_local, adj_boundary, occupancy):
    height = owned.shape[0]
    full_mask = expand(occupancy)
    local_tile = adj_local * full_mask[:, :height]
    edge_tile = adj_boundary * full_mask[:, height:]
    summed = jnp.dot(local_tile, owned, preferred_element_type=jnp.float32)
    summed = summed + jnp.dot(edge_tile, remote, preferred_element_type=jnp.float32)
    partial_value = lax.dot_general(
        edge_tile, owned, (((0,), (0,)), ((), ())), preferred_element_type=jnp.float32
    )
    return (summed, partial_value)


def body(
    features,
    history,
    new_owner,
    pull_rows,
    occupancy,
    adj_local,
    adj_boundary,
    w_first,
    bias_first,
    w_second,
    cotangent,
):
    peer_count = lax.axis_size("dev")
    height, breadth = features.shape
    cluster = height // peer_count
    pulled = pull_rows.shape[0]
    per_peer = pulled // peer_count
    indices = jnp.arange(peer_count, dtype=jnp.int32)
    matches = (new_owner[0][:, None] == indices[None, :]).astype(jnp.int32)
    inverse = jnp.sum(matches * indices[:, None], axis=0)

    def arrange(values):
        return values.reshape(peer_count, cluster, breadth)[inverse]

    requests = lax.all_to_all(
        pull_rows.reshape(peer_count, per_peer), "dev", split_axis=0, concat_axis=0, tiled=True
    ).reshape(pulled)

    def fetch_rows(values):
        return values[requests].reshape(peer_count, per_peer, breadth)

    selector = (requests[None, :] == jnp.arange(height, dtype=jnp.int32)[:, None]).astype(
        jnp.bfloat16
    )

    def collect(received):
        return jnp.dot(
            selector, received.reshape(pulled, breadth), preferred_element_type=jnp.float32
        )

    def layer_terms(owned, remote):
        return dense_terms(owned, remote, adj_local, adj_boundary, occupancy)

    moved_x, moved_h = (
        lax.all_to_all(arrange(features), "dev", split_axis=0, concat_axis=0, tiled=True),
        lax.all_to_all(arrange(history), "dev", split_axis=0, concat_axis=0, tiled=True),
    )
    own_x = moved_x.reshape(height, breadth)
    own_h = moved_h.reshape(height, breadth)
    far_x, far_h = (
        lax.all_to_all(fetch_rows(own_x), "dev", split_axis=0, concat_axis=0, tiled=True),
        lax.all_to_all(fetch_rows(own_h), "dev", split_axis=0, concat_axis=0, tiled=True),
    )
    summed_one, partial_one = layer_terms(own_x, far_x.reshape(pulled, breadth))
    pushed_one = lax.all_to_all(
        partial_one.astype(jnp.bfloat16).reshape(peer_count, per_peer, breadth),
        "dev",
        split_axis=0,
        concat_axis=0,
        tiled=True,
    )
    far_h = far_h.reshape(pulled, breadth)
    aggregate_one = (summed_one + collect(pushed_one)).astype(jnp.bfloat16)
    hidden = jnp.maximum(
        jnp.dot(aggregate_one, w_first, preferred_element_type=jnp.float32) + bias_first, 0.0
    ).astype(jnp.bfloat16)
    summed_two, partial_two = layer_terms(hidden, far_h)
    pushed_two = lax.all_to_all(
        partial_two.astype(jnp.bfloat16).reshape(peer_count, per_peer, breadth),
        "dev",
        split_axis=0,
        concat_axis=0,
        tiled=True,
    )
    aggregate_two = (summed_two + collect(pushed_two)).astype(jnp.bfloat16)
    output = jnp.dot(aggregate_two, w_second, preferred_element_type=jnp.float32).astype(
        jnp.bfloat16
    )
    local_grad = lax.dot_general(
        aggregate_two, cotangent, (((0,), (0,)), ((), ())), preferred_element_type=jnp.float32
    )
    gradient = lax.psum(local_grad, ("dev", "rep"))
    return (hidden, output, gradient)


def solution(mesh):
    return jax.shard_map(
        body,
        mesh=mesh,
        in_specs=(
            P(("dev", "rep"), None),
            P(("dev", "rep"), None),
            P(("dev", "rep"), None),
            P(("dev", "rep")),
            P(("dev", "rep"), None),
            P(("dev", "rep"), None),
            P(("dev", "rep"), None),
            P(),
            P(),
            P(),
            P(("dev", "rep"), None),
        ),
        out_specs=(P(("dev", "rep"), None), P(("dev", "rep"), None), P()),
        check_vma=False,
    )
```

profile of v0, /device:TPU:0, one launch (start us, length us, event | category | flops | bytes accessed | tf_op | source)
XLA Modules:
  0.0 263.3 jit_solution(17940252568643423680)
XLA Ops:
  7.2 7.5 %all-to-all-start.1 = ((s32[8,1,128]{2,1,0:T(1,128)}), s32[8,1,128]{2,1,0:T(1,128)S(1)}, u32[]{:S(2)}, u32[]{:S(2)}) async-start(s32[8,1,128]{2,1,0:T(1,128)} %bitcast.62), calls=%async_computation.1 | async-start | bytes 8192 | tf_op jit(solution)/shard_map/all_to_all | solution.py:49
  15.4 1.4 gather_fusion
  16.8 4.3 %all-to-all-done.1 = s32[8,1,128]{2,1,0:T(1,128)S(1)} async-done(((s32[8,1,128]{2,1,0:T(1,128)}), s32[8,1,128]{2,1,0:T(1,128)S(1)}, u32[]{:S(2)}, u32[]{:S(2)}) %all-to-all-start.1) | async-done | bytes 4128 | tf_op jit(solution)/shard_map/all_to_all | solution.py:49
  21.1 3.5 %all-to-all-start = ((bf16[8,128,256]{2,1,0:T(8,128)(2,1)}), bf16[8,128,256]{2,1,0:T(8,128)(2,1)S(1)}, u32[]{:S(2)}, u32[]{:S(2)}) async-start(bf16[8,128,256]{2,1,0:T(8,128)(2,1)} %gather_fusion), calls=%async_computation | async-start | bytes 1048576 | tf_op jit(solution)/shard_map/all_to_all | solution.py:69
  24.6 1.4 gather_fusion.2
  25.9 11.9 %all-to-all-done = bf16[8,128,256]{2,1,0:T(8,128)(2,1)S(1)} async-done(((bf16[8,128,256]{2,1,0:T(8,128)(2,1)}), bf16[8,128,256]{2,1,0:T(8,128)(2,1)S(1)}, u32[]{:S(2)}, u32[]{:S(2)}) %all-to-all-start) | async-done | bytes 524320 | tf_op jit(solution)/shard_map/all_to_all | solution.py:69
  37.8 3.7 %all-to-all-start.4 = ((bf16[8,128,256]{2,1,0:T(8,128)(2,1)}), bf16[8,128,256]{2,1,0:T(8,128)(2,1)S(1)}, u32[]{:S(2)}, u32[]{:S(2)}) async-start(bf16[8,128,256]{2,1,0:T(8,128)(2,1)} %gather_fusion.2), calls=%async_computation.4 | async-start | bytes 1048576 | tf_op jit(solution)/shard_map/all_to_all | solution.py:70
  41.5 5.0 %gather_fusion.1 = bf16[1024,256]{1,0:T(8,128)(2,1)} fusion(bf16[1024,256]{1,0:T(8,128)(2,1)S(1)} %bitcast.45, s32[1024]{0:T(1024)S(1)} %broadcast_clamp_fusion), kind=kCustom, calls=%fused_computation.1 | custom fusion | bytes 1052672 | tf_op jit(solution)/shard_map/gather | solution.py:54
  46.5 8.8 %all-to-all-done.4 = bf16[8,128,256]{2,1,0:T(8,128)(2,1)S(1)} async-done(((bf16[8,128,256]{2,1,0:T(8,128)(2,1)}), bf16[8,128,256]{2,1,0:T(8,128)(2,1)S(1)}, u32[]{:S(2)}, u32[]{:S(2)}) %all-to-all-start.4) | async-done | bytes 524320 | tf_op jit(solution)/shard_map/all_to_all | solution.py:70
  55.3 4.2 %all-to-all-start.2 = ((bf16[8,128,256]{2,1,0:T(8,128)(2,1)}), bf16[8,128,256]{2,1,0:T(8,128)(2,1)}, u32[]{:S(2)}, u32[]{:S(2)}) async-start(bf16[8,128,256]{2,1,0:T(8,128)(2,1)} %bitcast.9), calls=%async_computation.2 | async-start | bytes 1048576 | tf_op jit(solution)/shard_map/all_to_all | solution.py:75
  59.5 4.5 %broadcast_in_dim.5 = bf16[1024,16,128]{2,1,0:T(8,128)(2,1)S(1)} broadcast(bf16[1024,16]{1,0:T(8,128)(2,1)S(1)} %bitcast.55), dimensions={0,1} | broadcast | bytes 4227072 | tf_op jit(solution)/shard_map/broadcast_in_dim | solution.py:8
  64.0 2.2 copy.16
  66.4 1.7 copy-done.2
  68.1 1.6 convolution_convert_fusion.2
  69.7 3.5 %all-to-all-done.2 = bf16[8,128,256]{2,1,0:T(8,128)(2,1)} async-done(((bf16[8,128,256]{2,1,0:T(8,128)(2,1)}), bf16[8,128,256]{2,1,0:T(8,128)(2,1)}, u32[]{:S(2)}, u32[]{:S(2)}) %all-to-all-start.2) | async-done | bytes 524320 | tf_op jit(solution)/shard_map/all_to_all | solution.py:75
  73.2 4.1 %all-to-all-start.3 = ((bf16[8,128,256]{2,1,0:T(8,128)(2,1)}), bf16[8,128,256]{2,1,0:T(8,128)(2,1)}, u32[]{:S(2)}, u32[]{:S(2)}) async-start(bf16[8,128,256]{2,1,0:T(8,128)(2,1)} %bitcast.57), calls=%async_computation.3 | async-start | bytes 1048576 | tf_op jit(solution)/shard_map/all_to_all | solution.py:79
  77.4 5.7 %gather_fusion.3 = bf16[1024,256]{1,0:T(8,128)(2,1)} fusion(bf16[1024,256]{1,0:T(8,128)(2,1)} %bitcast.48, s32[1024]{0:T(1024)S(1)} %broadcast_clamp_fusion), kind=kCustom, calls=%fused_computation.3 | custom fusion | bytes 1052672 | tf_op jit(solution)/shard_map/gather | solution.py:54
  83.1 3.9 %fusion.11 = f32[1024,256]{1,0:T(8,128)} fusion(bf16[1024,256]{1,0:T(8,128)(2,1)S(1)} %bitcast.47, bf16[1024,1024]{1,0:T(8,128)(2,1)} %param.16, bf16[1024,2048]{1,0:T(8,128)(2,1)} %bitcast.51), kind=kOutput, calls=%fused_computation.25 | convolution fusion | flops 537919488 | bytes 5767168 | tf_op jit(solution)/shard_map/dot_general | solution.py:16
  87.0 3.7 %all-to-all-done.3 = bf16[8,128,256]{2,1,0:T(8,128)(2,1)} async-done(((bf16[8,128,256]{2,1,0:T(8,128)(2,1)}), bf16[8,128,256]{2,1,0:T(8,128)(2,1)}, u32[]{:S(2)}, u32[]{:S(2)}) %all-to-all-start.3) | async-done | bytes 524320 | tf_op jit(solution)/shard_map/all_to_all | solution.py:79
  90.7 3.7 %all-to-all-start.5 = ((bf16[8,128,256]{2,1,0:T(8,128)(2,1)}), bf16[8,128,256]{2,1,0:T(8,128)(2,1)S(1)}, u32[]{:S(2)}, u32[]{:S(2)}) async-start(bf16[8,128,256]{2,1,0:T(8,128)(2,1)} %bitcast.53), calls=%async_computation.5 | async-start | bytes 1048576 | tf_op jit(solution)/shard_map/all_to_all | solution.py:76
  94.4 3.1 %convolution_add_fusion.2 = f32[1024,256]{1,0:T(8,128)} fusion(f32[1024,256]{1,0:T(8,128)} %fusion.11, bf16[1024,1024]{1,0:T(8,128)(2,1)S(1)} %slice_multiply_fusion, bf16[1024,256]{1,0:T(8,128)(2,1)} %bitcast.10), kind=kOutput, calls=%fused_computation.17 | convolution fusion | flops 537133056 | bytes 4718592 | tf_op jit(solution)/shard_map/dot_general | solution.py:17
  97.5 3.2 %fusion.7 = bf16[1024,256]{1,0:T(8,128)(2,1)} fusion(bf16[256,256]{1,0:T(8,128)(2,1)S(1)} %copy-done.8, f32[1024,256]{1,0:T(8,128)} %convolution_add_fusion.2, bf16[1024,256]{1,0:T(8,128)(2,1)} %bitcast.13, s32[1024]{0:T(1024)S(1)} %bitcast.59, f32[256]{0:T(256)S(1)} %copy-done.9), kind=kOutput, calls=%fused_computation.18 | convolution fusion | flops 673447936 | bytes 2233344 | tf_op jit(solution)/shard_map/dot_general | solution.py:89
  100.7 2.6 convolution_convert_fusion.1
  103.3 4.8 %all-to-all-done.5 = bf16[8,128,256]{2,1,0:T(8,128)(2,1)S(1)} async-done(((bf16[8,128,256]{2,1,0:T(8,128)(2,1)}), bf16[8,128,256]{2,1,0:T(8,128)(2,1)S(1)}, u32[]{:S(2)}, u32[]{:S(2)}) %all-to-all-start.5) | async-done | bytes 524320 | tf_op jit(solution)/shard_map/all_to_all | solution.py:76
  108.2 4.1 %all-to-all-start.6 = ((bf16[8,128,256]{2,1,0:T(8,128)(2,1)}), bf16[8,128,256]{2,1,0:T(8,128)(2,1)}, u32[]{:S(2)}, u32[]{:S(2)}) async-start(bf16[8,128,256]{2,1,0:T(8,128)(2,1)} %bitcast.56), calls=%async_computation.6 | async-start | bytes 1048576 | tf_op jit(solution)/shard_map/all_to_all | solution.py:92
  112.5 3.0 %fusion.10 = f32[1024,256]{1,0:T(8,128)S(1)} fusion(bf16[1024,256]{1,0:T(8,128)(2,1)} %fusion.7, bf16[1024,1024]{1,0:T(8,128)(2,1)} %param.16, bf16[1024,2048]{1,0:T(8,128)(2,1)} %bitcast.52), kind=kOutput, calls=%fused_computation.24 | convolution fusion | flops 537919488 | bytes 5767168 | tf_op jit(solution)/shard_map/dot_general | solution.py:16
  115.6 1.7 convolution_add_fusion.1
  117.3 8.4 %all-to-all-done.6 = bf16[8,128,256]{2,1,0:T(8,128)(2,1)} async-done(((bf16[8,128,256]{2,1,0:T(8,128)(2,1)}), bf16[8,128,256]{2,1,0:T(8,128)(2,1)}, u32[]{:S(2)}, u32[]{:S(2)}) %all-to-all-start.6) | async-done | bytes 524320 | tf_op jit(solution)/shard_map/all_to_all | solution.py:92
  125.7 2.2 fusion.8
  129.0 1.1 convolution_convert_fusion
  130.1 124.7 %all-reduce.2.cloned.1.call-done = f32[256,256]{1,0:T(8,128)} async-done(((f32[256,256]{1,0:T(8,128)}), f32[256,256]{1,0:T(8,128)}) %all-reduce.2.cloned.1.call-update) | async-done | bytes 262160 | tf_op jit(solution)/shard_map/psum | solution.py:106
  254.8 1.7 copy.18
  (30 shorter events, 2.4 us)
Async XLA Ops:
  7.2 8.2 %copy-start = (bf16[1024,256]{1,0:T(8,128)(2,1)S(1)}, bf16[1024,256]{1,0:T(8,128)(2,1)}, u32[]{:S(2)}) copy-start(bf16[1024,256]{1,0:T(8,128)(2,1)} %param.11) | copy-start | bytes 1572868
  7.2 17.4 %copy-start.5 = (bf16[1024,256]{1,0:T(8,128)(2,1)S(1)}, bf16[1024,256]{1,0:T(8,128)(2,1)}, u32[]{:S(2)}) copy-start(bf16[1024,256]{1,0:T(8,128)(2,1)} %param.12) | copy-start | bytes 1572868
  7.2 13.9 %all-to-all-start.1 = ((s32[8,1,128]{2,1,0:T(1,128)}), s32[8,1,128]{2,1,0:T(1,128)S(1)}, u32[]{:S(2)}, u32[]{:S(2)}) async-start(s32[8,1,128]{2,1,0:T(1,128)} %bitcast.62), calls=%async_computation.1 | async-start | bytes 8192 | tf_op jit(solution)/shard_map/all_to_all | solution.py:49
  21.1 16.8 %all-to-all-start = ((bf16[8,128,256]{2,1,0:T(8,128)(2,1)}), bf16[8,128,256]{2,1,0:T(8,128)(2,1)S(1)}, u32[]{:S(2)}, u32[]{:S(2)}) async-start(bf16[8,128,256]{2,1,0:T(8,128)(2,1)} %gather_fusion), calls=%async_computation | async-start | bytes 1048576 | tf_op jit(solution)/shard_map/all_to_all | solution.py:69
  37.8 17.5 %all-to-all-start.4 = ((bf16[8,128,256]{2,1,0:T(8,128)(2,1)}), bf16[8,128,256]{2,1,0:T(8,128)(2,1)S(1)}, u32[]{:S(2)}, u32[]{:S(2)}) async-start(bf16[8,128,256]{2,1,0:T(8,128)(2,1)} %gather_fusion.2), calls=%async_computation.4 | async-start | bytes 1048576 | tf_op jit(solution)/shard_map/all_to_all | solution.py:70
  41.5 18.0 %copy-start.7 = (s32[8,16]{1,0:T(8,128)S(1)}, s32[8,16]{1,0:T(8,128)}, u32[]{:S(2)}) copy-start(s32[8,16]{1,0:T(8,128)} %param.15) | copy-start | bytes 1540
  55.3 8.7 %copy-start.1 = (bf16[8,128,256]{2,1,0:T(8,128)(2,1)}, bf16[8,128,256]{2,1,0:T(8,128)(2,1)S(1)}, u32[]{:S(2)}) copy-start(bf16[8,128,256]{2,1,0:T(8,128)(2,1)S(1)} %all-to-all-done.4) | copy-start | bytes 1572868
  55.3 17.9 %all-to-all-start.2 = ((bf16[8,128,256]{2,1,0:T(8,128)(2,1)}), bf16[8,128,256]{2,1,0:T(8,128)(2,1)}, u32[]{:S(2)}, u32[]{:S(2)}) async-start(bf16[8,128,256]{2,1,0:T(8,128)(2,1)} %bitcast.9), calls=%async_computation.2 | async-start | bytes 1048576 | tf_op jit(solution)/shard_map/all_to_all | solution.py:75
  64.0 2.2 copy-start.3
  66.2 1.9 copy-start.2
  73.2 17.5 %all-to-all-start.3 = ((bf16[8,128,256]{2,1,0:T(8,128)(2,1)}), bf16[8,128,256]{2,1,0:T(8,128)(2,1)}, u32[]{:S(2)}, u32[]{:S(2)}) async-start(bf16[8,128,256]{2,1,0:T(8,128)(2,1)} %bitcast.57), calls=%async_computation.3 | async-start | bytes 1048576 | tf_op jit(solution)/shard_map/all_to_all | solution.py:79
  90.7 17.5 %all-to-all-start.5 = ((bf16[8,128,256]{2,1,0:T(8,128)(2,1)}), bf16[8,128,256]{2,1,0:T(8,128)(2,1)S(1)}, u32[]{:S(2)}, u32[]{:S(2)}) async-start(bf16[8,128,256]{2,1,0:T(8,128)(2,1)} %bitcast.53), calls=%async_computation.5 | async-start | bytes 1048576 | tf_op jit(solution)/shard_map/all_to_all | solution.py:76
  94.4 3.1 %copy-start.8 = (bf16[256,256]{1,0:T(8,128)(2,1)S(1)}, bf16[256,256]{1,0:T(8,128)(2,1)}, u32[]{:S(2)}) copy-start(bf16[256,256]{1,0:T(8,128)(2,1)} %param.18) | copy-start | bytes 393220
  94.4 3.1 %copy-start.9 = (f32[256]{0:T(256)S(1)}, f32[256]{0:T(256)}, u32[]{:S(2)}) copy-start(f32[256]{0:T(256)} %param.19) | copy-start | bytes 3076
  108.2 17.5 %all-to-all-start.6 = ((bf16[8,128,256]{2,1,0:T(8,128)(2,1)}), bf16[8,128,256]{2,1,0:T(8,128)(2,1)}, u32[]{:S(2)}, u32[]{:S(2)}) async-start(bf16[8,128,256]{2,1,0:T(8,128)(2,1)} %bitcast.56), calls=%async_computation.6 | async-start | bytes 1048576 | tf_op jit(solution)/shard_map/all_to_all | solution.py:92
  112.3 142.5 %all-reduce.2.cloned.1.call-start = ((), (), s32[]{:S(2)}) async-start(), calls=%async_computation.7 | async-start | bytes 524288 | tf_op jit(solution)/shard_map/psum | solution.py:106
  117.3 10.7 %copy-start.4 = (bf16[1024,256]{1,0:T(8,128)(2,1)S(1)}, bf16[1024,256]{1,0:T(8,128)(2,1)}, u32[]{:S(2)}) copy-start(bf16[1024,256]{1,0:T(8,128)(2,1)} %param.21) | copy-start | bytes 1572868
  125.7 3.3 %copy-start.6 = (bf16[256,256]{1,0:T(8,128)(2,1)S(1)}, bf16[256,256]{1,0:T(8,128)(2,1)}, u32[]{:S(2)}) copy-start(bf16[256,256]{1,0:T(8,128)(2,1)} %param.20) | copy-start | bytes 393220
Sparse Core Ops, SparseCore 0:
  129.1 125.6 all-reduce.1
where the time goes:
time: 264 us; the launch traced here: 263 us
  waiting for transfers between devices  170 us (64%)
  starting transfers between devices  31 us (12%)
  local copies, waits for them, and re-layouts  23.5 us (9%)
  matrix products  23.5 us (9%)
  between operations  14.2 us (5%)
    psum x1, waiting for transfers between devices, body(): gradient = lax.psum(local_grad, ('dev', 'rep'))  125 us
    all_to_all x1, waiting for transfers between devices, body(): lax.all_to_all(arrange(features), 'dev', split_axis=0, concat_axis=0, til...  11.9 us
    gather x2, local copies, waits for them, and re-layouts, fetch_rows(): return values[requests].reshape(peer_count, per_peer, breadth)  10.7 us
    all_to_all x1, waiting for transfers between devices, body(): lax.all_to_all(arrange(history), 'dev', split_axis=0, concat_axis=0, tile...  8.81 us
    all_to_all x1, waiting for transfers between devices, body(): lax.all_to_all(partial_two.astype(jnp.bfloat16).reshape(peer_count, per_p...  8.41 us
    all_to_all x1, starting transfers between devices, body(): lax.all_to_all(pull_rows.reshape(peer_count, per_peer), 'dev', split_axis...  7.45 us
    dot_general x2, matrix products, dense_terms(): summed = jnp.dot(local_tile, owned, preferred_element_type=jnp.float32)  6.92 us
    unnamed x22, local copies, waits for them, and re-layouts  5.58 us
  transfers between devices with their start and end apart: 8, of which 8 were waited for; matrix products, arithmetic and copies ran while one was open for 16% of the time, Pallas kernels for 0%

commit v1 on v0

--- a/solution.py
+++ b/solution.py
@@ -103,7 +103,7 @@
     local_grad = lax.dot_general(
         aggregate_two, cotangent, (((0,), (0,)), ((), ())), preferred_element_type=jnp.float32
     )
-    gradient = lax.psum(local_grad, ("dev", "rep"))
+    gradient = jnp.sum(lax.all_gather(local_grad, ("dev", "rep")), axis=0)
     return (hidden, output, gradient)
 
 

time: 264 us -> 218 us (0.83)
  waiting for transfers between devices: 170 us -> 121 us
  other arithmetic: 0.98 us -> 5.61 us
    psum x1 -> x0, waiting for transfers between devices: 125 us -> none  [body(): gradient = lax.psum(local_grad, ('dev', 'rep'))]
    all_gather x0 -> x1, waiting for transfers between devices: none -> 75.2 us  [body(): gradient = jnp.sum(lax.all_gather(local_grad, ('dev', 'rep')), axis=0)]
    reduce_sum x0 -> x1, other arithmetic: none -> 4.63 us  [body(): gradient = jnp.sum(lax.all_gather(local_grad, ('dev', 'rep')), axis=0)]
    unnamed x22 -> x21, local copies, waits for them, and re-layouts: 5.58 us -> 3.91 us
  transfers between devices with their start and end apart: 8 -> 8, of which waited for: 8 -> 8; matrix products, arithmetic and copies ran while one was open for 16% -> 19% of each run, Pallas kernels for 0% -> 0%
where the time goes in v1:
time: 218 us; the launch traced here: 217 us
  waiting for transfers between devices  121 us (56%)
  starting transfers between devices  31 us (14%)
  matrix products  23.5 us (11%)
  local copies, waits for them, and re-layouts  21.9 us (10%)
  between operations  14.2 us (7%)
  other arithmetic  5.61 us (3%)
    all_gather x1, waiting for transfers between devices, body(): gradient = jnp.sum(lax.all_gather(local_grad, ('dev', 'rep')), axis=0)  75.2 us
    all_to_all x1, waiting for transfers between devices, body(): lax.all_to_all(arrange(features), 'dev', split_axis=0, concat_axis=0, til...  11.9 us
    gather x2, local copies, waits for them, and re-layouts, fetch_rows(): return values[requests].reshape(peer_count, per_peer, breadth)  10.7 us
    all_to_all x1, waiting for transfers between devices, body(): lax.all_to_all(arrange(history), 'dev', split_axis=0, concat_axis=0, tile...  8.81 us
    all_to_all x1, waiting for transfers between devices, body(): lax.all_to_all(partial_two.astype(jnp.bfloat16).reshape(peer_count, per_p...  8.41 us
    all_to_all x1, starting transfers between devices, body(): lax.all_to_all(pull_rows.reshape(peer_count, per_peer), 'dev', split_axis...  7.45 us
    dot_general x2, matrix products, dense_terms(): summed = jnp.dot(local_tile, owned, preferred_element_type=jnp.float32)  6.91 us
    all_to_all x1, waiting for transfers between devices, body(): lax.all_to_all(fetch_rows(own_h), 'dev', split_axis=0, concat_axis=0, til...  4.85 us
  transfers between devices with their start and end apart: 8, of which 8 were waited for; matrix products, arithmetic and copies ran while one was open for 19% of the time, Pallas kernels for 0%

profile of v1, /device:TPU:0, one launch (start us, length us, event | category | flops | bytes accessed | tf_op | source)
XLA Modules:
  0.0 216.8 jit_solution(16556854404453820151)
XLA Ops:
  7.2 7.5 %all-to-all-start.1 = ((s32[8,1,128]{2,1,0:T(1,128)}), s32[8,1,128]{2,1,0:T(1,128)S(1)}, u32[]{:S(2)}, u32[]{:S(2)}) async-start(s32[8,1,128]{2,1,0:T(1,128)} %bitcast.64), calls=%async_computation.1 | async-start | bytes 8192 | tf_op jit(solution)/shard_map/all_to_all | solution.py:49
  15.4 1.4 gather_fusion
  16.8 4.3 %all-to-all-done.1 = s32[8,1,128]{2,1,0:T(1,128)S(1)} async-done(((s32[8,1,128]{2,1,0:T(1,128)}), s32[8,1,128]{2,1,0:T(1,128)S(1)}, u32[]{:S(2)}, u32[]{:S(2)}) %all-to-all-start.1) | async-done | bytes 4128 | tf_op jit(solution)/shard_map/all_to_all | solution.py:49
  21.1 3.5 %all-to-all-start = ((bf16[8,128,256]{2,1,0:T(8,128)(2,1)}), bf16[8,128,256]{2,1,0:T(8,128)(2,1)S(1)}, u32[]{:S(2)}, u32[]{:S(2)}) async-start(bf16[8,128,256]{2,1,0:T(8,128)(2,1)} %gather_fusion), calls=%async_computation | async-start | bytes 1048576 | tf_op jit(solution)/shard_map/all_to_all | solution.py:69
  24.6 1.4 gather_fusion.2
  25.9 11.9 %all-to-all-done = bf16[8,128,256]{2,1,0:T(8,128)(2,1)S(1)} async-done(((bf16[8,128,256]{2,1,0:T(8,128)(2,1)}), bf16[8,128,256]{2,1,0:T(8,128)(2,1)S(1)}, u32[]{:S(2)}, u32[]{:S(2)}) %all-to-all-start) | async-done | bytes 524320 | tf_op jit(solution)/shard_map/all_to_all | solution.py:69
  37.8 3.7 %all-to-all-start.4 = ((bf16[8,128,256]{2,1,0:T(8,128)(2,1)}), bf16[8,128,256]{2,1,0:T(8,128)(2,1)S(1)}, u32[]{:S(2)}, u32[]{:S(2)}) async-start(bf16[8,128,256]{2,1,0:T(8,128)(2,1)} %gather_fusion.2), calls=%async_computation.4 | async-start | bytes 1048576 | tf_op jit(solution)/shard_map/all_to_all | solution.py:70
  41.5 5.0 %gather_fusion.1 = bf16[1024,256]{1,0:T(8,128)(2,1)} fusion(bf16[1024,256]{1,0:T(8,128)(2,1)S(1)} %bitcast.46, s32[1024]{0:T(1024)S(1)} %broadcast_clamp_fusion), kind=kCustom, calls=%fused_computation.1 | custom fusion | bytes 1052672 | tf_op jit(solution)/shard_map/gather | solution.py:54
  46.5 8.8 %all-to-all-done.4 = bf16[8,128,256]{2,1,0:T(8,128)(2,1)S(1)} async-done(((bf16[8,128,256]{2,1,0:T(8,128)(2,1)}), bf16[8,128,256]{2,1,0:T(8,128)(2,1)S(1)}, u32[]{:S(2)}, u32[]{:S(2)}) %all-to-all-start.4) | async-done | bytes 524320 | tf_op jit(solution)/shard_map/all_to_all | solution.py:70
  55.3 4.2 %all-to-all-start.2 = ((bf16[8,128,256]{2,1,0:T(8,128)(2,1)}), bf16[8,128,256]{2,1,0:T(8,128)(2,1)}, u32[]{:S(2)}, u32[]{:S(2)}) async-start(bf16[8,128,256]{2,1,0:T(8,128)(2,1)} %bitcast.9), calls=%async_computation.2 | async-start | bytes 1048576 | tf_op jit(solution)/shard_map/all_to_all | solution.py:75
  59.5 4.5 %broadcast_in_dim.5 = bf16[1024,16,128]{2,1,0:T(8,128)(2,1)S(1)} broadcast(bf16[1024,16]{1,0:T(8,128)(2,1)S(1)} %bitcast.57), dimensions={0,1} | broadcast | bytes 4227072 | tf_op jit(solution)/shard_map/broadcast_in_dim | solution.py:8
  64.0 2.2 copy.16
  66.4 1.7 copy-done.2
  68.1 1.6 convolution_convert_fusion.2
  69.7 3.5 %all-to-all-done.2 = bf16[8,128,256]{2,1,0:T(8,128)(2,1)} async-done(((bf16[8,128,256]{2,1,0:T(8,128)(2,1)}), bf16[8,128,256]{2,1,0:T(8,128)(2,1)}, u32[]{:S(2)}, u32[]{:S(2)}) %all-to-all-start.2) | async-done | bytes 524320 | tf_op jit(solution)/shard_map/all_to_all | solution.py:75
  73.2 4.1 %all-to-all-start.3 = ((bf16[8,128,256]{2,1,0:T(8,128)(2,1)}), bf16[8,128,256]{2,1,0:T(8,128)(2,1)}, u32[]{:S(2)}, u32[]{:S(2)}) async-start(bf16[8,128,256]{2,1,0:T(8,128)(2,1)} %bitcast.59), calls=%async_computation.3 | async-start | bytes 1048576 | tf_op jit(solution)/shard_map/all_to_all | solution.py:79
  77.4 5.7 %gather_fusion.3 = bf16[1024,256]{1,0:T(8,128)(2,1)} fusion(bf16[1024,256]{1,0:T(8,128)(2,1)} %bitcast.49, s32[1024]{0:T(1024)S(1)} %broadcast_clamp_fusion), kind=kCustom, calls=%fused_computation.3 | custom fusion | bytes 1052672 | tf_op jit(solution)/shard_map/gather | solution.py:54
  83.1 3.9 %fusion.11 = f32[1024,256]{1,0:T(8,128)} fusion(bf16[1024,256]{1,0:T(8,128)(2,1)S(1)} %bitcast.48, bf16[1024,1024]{1,0:T(8,128)(2,1)} %param.16, bf16[1024,2048]{1,0:T(8,128)(2,1)} %bitcast.52), kind=kOutput, calls=%fused_computation.25 | convolution fusion | flops 537919488 | bytes 5767168 | tf_op jit(solution)/shard_map/dot_general | solution.py:16
  87.0 3.7 %all-to-all-done.3 = bf16[8,128,256]{2,1,0:T(8,128)(2,1)} async-done(((bf16[8,128,256]{2,1,0:T(8,128)(2,1)}), bf16[8,128,256]{2,1,0:T(8,128)(2,1)}, u32[]{:S(2)}, u32[]{:S(2)}) %all-to-all-start.3) | async-done | bytes 524320 | tf_op jit(solution)/shard_map/all_to_all | solution.py:79
  90.7 3.7 %all-to-all-start.5 = ((bf16[8,128,256]{2,1,0:T(8,128)(2,1)}), bf16[8,128,256]{2,1,0:T(8,128)(2,1)S(1)}, u32[]{:S(2)}, u32[]{:S(2)}) async-start(bf16[8,128,256]{2,1,0:T(8,128)(2,1)} %bitcast.55), calls=%async_computation.5 | async-start | bytes 1048576 | tf_op jit(solution)/shard_map/all_to_all | solution.py:76
  94.4 3.1 %convolution_add_fusion.2 = f32[1024,256]{1,0:T(8,128)} fusion(f32[1024,256]{1,0:T(8,128)} %fusion.11, bf16[1024,1024]{1,0:T(8,128)(2,1)S(1)} %slice_multiply_fusion, bf16[1024,256]{1,0:T(8,128)(2,1)} %bitcast.10), kind=kOutput, calls=%fused_computation.17 | convolution fusion | flops 537133056 | bytes 4718592 | tf_op jit(solution)/shard_map/dot_general | solution.py:17
  97.5 3.2 %fusion.7 = bf16[1024,256]{1,0:T(8,128)(2,1)} fusion(bf16[256,256]{1,0:T(8,128)(2,1)S(1)} %copy-done.8, f32[1024,256]{1,0:T(8,128)} %convolution_add_fusion.2, bf16[1024,256]{1,0:T(8,128)(2,1)} %bitcast.13, s32[1024]{0:T(1024)S(1)} %bitcast.61, f32[256]{0:T(256)S(1)} %copy-done.9), kind=kOutput, calls=%fused_computation.18 | convolution fusion | flops 673447936 | bytes 2233344 | tf_op jit(solution)/shard_map/dot_general | solution.py:89
  100.7 2.6 %convolution_convert_fusion.1 = bf16[1024,256]{1,0:T(8,128)(2,1)} fusion(bf16[1024,1024]{1,0:T(8,128)(2,1)S(1)} %slice_multiply_fusion, bf16[1024,256]{1,0:T(8,128)(2,1)} %fusion.7), kind=kOutput, calls=%fused_computation.22 | convolution fusion | flops 537133056 | bytes 3145728 | tf_op jit(solution)/shard_map/dot_general | solution.py:18
  103.3 4.8 %all-to-all-done.5 = bf16[8,128,256]{2,1,0:T(8,128)(2,1)S(1)} async-done(((bf16[8,128,256]{2,1,0:T(8,128)(2,1)}), bf16[8,128,256]{2,1,0:T(8,128)(2,1)S(1)}, u32[]{:S(2)}, u32[]{:S(2)}) %all-to-all-start.5) | async-done | bytes 524320 | tf_op jit(solution)/shard_map/all_to_all | solution.py:76
  108.2 4.1 %all-to-all-start.6 = ((bf16[8,128,256]{2,1,0:T(8,128)(2,1)}), bf16[8,128,256]{2,1,0:T(8,128)(2,1)}, u32[]{:S(2)}, u32[]{:S(2)}) async-start(bf16[8,128,256]{2,1,0:T(8,128)(2,1)} %bitcast.58), calls=%async_computation.6 | async-start | bytes 1048576 | tf_op jit(solution)/shard_map/all_to_all | solution.py:92
  112.5 3.0 %fusion.10 = f32[1024,256]{1,0:T(8,128)S(1)} fusion(bf16[1024,256]{1,0:T(8,128)(2,1)} %fusion.7, bf16[1024,1024]{1,0:T(8,128)(2,1)} %param.16, bf16[1024,2048]{1,0:T(8,128)(2,1)} %bitcast.53), kind=kOutput, calls=%fused_computation.24 | convolution fusion | flops 537919488 | bytes 5767168 | tf_op jit(solution)/shard_map/dot_general | solution.py:16
  115.6 1.7 convolution_add_fusion.1
  117.3 8.4 %all-to-all-done.6 = bf16[8,128,256]{2,1,0:T(8,128)(2,1)} async-done(((bf16[8,128,256]{2,1,0:T(8,128)(2,1)}), bf16[8,128,256]{2,1,0:T(8,128)(2,1)}, u32[]{:S(2)}, u32[]{:S(2)}) %all-to-all-start.6) | async-done | bytes 524320 | tf_op jit(solution)/shard_map/all_to_all | solution.py:92
  125.7 2.2 %fusion.8 = bf16[1024,256]{1,0:T(8,128)(2,1)S(1)} fusion(f32[1024,256]{1,0:T(8,128)} %convolution_add_fusion.1, bf16[1024,256]{1,0:T(8,128)(2,1)} %bitcast.19, s32[1024]{0:T(1024)S(1)} %bitcast.62), kind=kOutput, calls=%fused_computation.20 | convolution fusion | flops 538443776 | bytes 2101248 | tf_op jit(solution)/shard_map/dot_general | solution.py:61
  129.0 1.1 convolution_convert_fusion
  130.1 75.2 %all-gather.3.cloned.1.call-done = f32[8192,256]{1,0:T(8,128)} async-done(((f32[256,256]{1,0:T(8,128)}), f32[8192,256]{1,0:T(8,128)}) %all-gather.3.cloned.1.call-update) | async-done | bytes 8388624 | tf_op jit(solution)/shard_map/all_gather | solution.py:106
  205.3 4.6 %reduce_sum.22 = f32[256,256]{1,0:T(8,128)} reduce(f32[32,256,256]{2,1,0:T(8,128)} %bitcast.54, f32[]{:T(128)} %constant.1.clone.1), dimensions={0}, to_apply=%region_1.0 | reduce | flops 2031616 | bytes 8650756 | tf_op jit(solution)/shard_map/reduce_sum | solution.py:106
  (30 shorter events, 2.4 us)
Async XLA Ops:
  7.2 8.2 %copy-start = (bf16[1024,256]{1,0:T(8,128)(2,1)S(1)}, bf16[1024,256]{1,0:T(8,128)(2,1)}, u32[]{:S(2)}) copy-start(bf16[1024,256]{1,0:T(8,128)(2,1)} %param.11) | copy-start | bytes 1572868
  7.2 17.4 %copy-start.5 = (bf16[1024,256]{1,0:T(8,128)(2,1)S(1)}, bf16[1024,256]{1,0:T(8,128)(2,1)}, u32[]{:S(2)}) copy-start(bf16[1024,256]{1,0:T(8,128)(2,1)} %param.12) | copy-start | bytes 1572868
  7.2 13.9 %all-to-all-start.1 = ((s32[8,1,128]{2,1,0:T(1,128)}), s32[8,1,128]{2,1,0:T(1,128)S(1)}, u32[]{:S(2)}, u32[]{:S(2)}) async-start(s32[8,1,128]{2,1,0:T(1,128)} %bitcast.64), calls=%async_computation.1 | async-start | bytes 8192 | tf_op jit(solution)/shard_map/all_to_all | solution.py:49
  21.1 16.8 %all-to-all-start = ((bf16[8,128,256]{2,1,0:T(8,128)(2,1)}), bf16[8,128,256]{2,1,0:T(8,128)(2,1)S(1)}, u32[]{:S(2)}, u32[]{:S(2)}) async-start(bf16[8,128,256]{2,1,0:T(8,128)(2,1)} %gather_fusion), calls=%async_computation | async-start | bytes 1048576 | tf_op jit(solution)/shard_map/all_to_all | solution.py:69
  37.8 17.5 %all-to-all-start.4 = ((bf16[8,128,256]{2,1,0:T(8,128)(2,1)}), bf16[8,128,256]{2,1,0:T(8,128)(2,1)S(1)}, u32[]{:S(2)}, u32[]{:S(2)}) async-start(bf16[8,128,256]{2,1,0:T(8,128)(2,1)} %gather_fusion.2), calls=%async_computation.4 | async-start | bytes 1048576 | tf_op jit(solution)/shard_map/all_to_all | solution.py:70
  41.5 18.0 %copy-start.7 = (s32[8,16]{1,0:T(8,128)S(1)}, s32[8,16]{1,0:T(8,128)}, u32[]{:S(2)}) copy-start(s32[8,16]{1,0:T(8,128)} %param.15) | copy-start | bytes 1540
  55.3 8.7 %copy-start.1 = (bf16[8,128,256]{2,1,0:T(8,128)(2,1)}, bf16[8,128,256]{2,1,0:T(8,128)(2,1)S(1)}, u32[]{:S(2)}) copy-start(bf16[8,128,256]{2,1,0:T(8,128)(2,1)S(1)} %all-to-all-done.4) | copy-start | bytes 1572868
  55.3 17.9 %all-to-all-start.2 = ((bf16[8,128,256]{2,1,0:T(8,128)(2,1)}), bf16[8,128,256]{2,1,0:T(8,128)(2,1)}, u32[]{:S(2)}, u32[]{:S(2)}) async-start(bf16[8,128,256]{2,1,0:T(8,128)(2,1)} %bitcast.9), calls=%async_computation.2 | async-start | bytes 1048576 | tf_op jit(solution)/shard_map/all_to_all | solution.py:75
  64.0 2.2 %copy-start.3 = (bf16[1024,1024]{1,0:T(8,128)(2,1)S(1)}, bf16[1024,1024]{1,0:T(8,128)(2,1)}, u32[]{:S(2)}) copy-start(bf16[1024,1024]{1,0:T(8,128)(2,1)} %param.17) | copy-start | bytes 6291460
  66.2 1.9 copy-start.2
  73.2 17.5 %all-to-all-start.3 = ((bf16[8,128,256]{2,1,0:T(8,128)(2,1)}), bf16[8,128,256]{2,1,0:T(8,128)(2,1)}, u32[]{:S(2)}, u32[]{:S(2)}) async-start(bf16[8,128,256]{2,1,0:T(8,128)(2,1)} %bitcast.59), calls=%async_computation.3 | async-start | bytes 1048576 | tf_op jit(solution)/shard_map/all_to_all | solution.py:79
  90.7 17.5 %all-to-all-start.5 = ((bf16[8,128,256]{2,1,0:T(8,128)(2,1)}), bf16[8,128,256]{2,1,0:T(8,128)(2,1)S(1)}, u32[]{:S(2)}, u32[]{:S(2)}) async-start(bf16[8,128,256]{2,1,0:T(8,128)(2,1)} %bitcast.55), calls=%async_computation.5 | async-start | bytes 1048576 | tf_op jit(solution)/shard_map/all_to_all | solution.py:76
  94.4 3.1 %copy-start.8 = (bf16[256,256]{1,0:T(8,128)(2,1)S(1)}, bf16[256,256]{1,0:T(8,128)(2,1)}, u32[]{:S(2)}) copy-start(bf16[256,256]{1,0:T(8,128)(2,1)} %param.18) | copy-start | bytes 393220
  94.4 3.1 %copy-start.9 = (f32[256]{0:T(256)S(1)}, f32[256]{0:T(256)}, u32[]{:S(2)}) copy-start(f32[256]{0:T(256)} %param.19) | copy-start | bytes 3076
  108.2 17.5 %all-to-all-start.6 = ((bf16[8,128,256]{2,1,0:T(8,128)(2,1)}), bf16[8,128,256]{2,1,0:T(8,128)(2,1)}, u32[]{:S(2)}, u32[]{:S(2)}) async-start(bf16[8,128,256]{2,1,0:T(8,128)(2,1)} %bitcast.58), calls=%async_computation.6 | async-start | bytes 1048576 | tf_op jit(solution)/shard_map/all_to_all | solution.py:92
  112.3 93.0 %all-gather.3.cloned.1.call-start = ((), (), s32[]{:S(2)}) async-start(), calls=%async_computation.7 | async-start | bytes 8650752 | tf_op jit(solution)/shard_map/all_gather | solution.py:106
  117.3 10.7 %copy-start.4 = (bf16[1024,256]{1,0:T(8,128)(2,1)S(1)}, bf16[1024,256]{1,0:T(8,128)(2,1)}, u32[]{:S(2)}) copy-start(bf16[1024,256]{1,0:T(8,128)(2,1)} %param.21) | copy-start | bytes 1572868
  125.7 3.3 %copy-start.6 = (bf16[256,256]{1,0:T(8,128)(2,1)S(1)}, bf16[256,256]{1,0:T(8,128)(2,1)}, u32[]{:S(2)}) copy-start(bf16[256,256]{1,0:T(8,128)(2,1)} %param.20) | copy-start | bytes 393220
Sparse Core Ops, SparseCore 0:
  129.1 76.1 all-gather.2
